TPU v7x, 32 devices: a whole 2x2x4 slice. The times are simulated.
32 devices in a mesh: rep: 4 (over x, core), dp: 4 (over z), tp: 2 (over y).
Axes of the slice: x: 2, y: 2, z: 4, core: 2. Of those that a mesh axis runs over, the one named last changes fastest.
Arguments:
- hidden: bfloat16 [4, 512, 14336], P('rep', None, 'tp'), may hold values from -6 to 6
- down_weight: bfloat16 [14336, 8192], P('tp', 'dp'), may hold values from -0.046875 to 0.046875
- out_grad: bfloat16 [4, 512, 8192], P('rep', 'tp', 'dp'), may hold values from -6 to 6
- pseudo_grad: bfloat16 [4, 14336, 8192], P('rep', 'tp', 'dp'), may hold values from -6 to 6
- momentum: float32 [14336, 8192], P(('tp', 'rep'), 'dp'), may hold values from -6 to 6
Outputs:
- layer_out: bfloat16 [4, 512, 8192], P('rep', 'tp', 'dp')
- hidden_grad: bfloat16 [4, 512, 14336], P('rep', 'dp', 'tp')
- new_momentum: float32 [14336, 8192], P(('tp', 'rep'), 'dp')
- outer_step: bfloat16 [14336, 8192], P('tp', 'dp')
All inputs are finite; a program needn't handle non-finite values.
Results may differ from a plain program's by a relative error of at most 0.017.
Values may be sent and summed in bfloat16 or wider, within the bound.
A program may use at most 256 MiB of HBM per device.

v0:
```python
import jax
import jax.numpy as jnp
from jax import lax
from jax.sharding import PartitionSpec as P

outer_rate = 0.7
momentum_rate = 0.9


def per_device(hidden, down_weight, out_grad, pseudo_grad, momentum):
    token_rows = hidden[0]
    local_grads = out_grad[0]
    row_block = token_rows
    layer_out = lax.psum_scatter(
        jnp.dot(row_block, down_weight, preferred_element_type=jnp.float32).astype(jnp.bfloat16),
        "tp",
        scatter_dimension=0,
        tiled=True,
    )
    all_grads = lax.all_gather(local_grads, "tp", axis=0, tiled=True)
    row_block = all_grads
    hidden_grad = lax.psum_scatter(
        lax.dot_general(
            row_block, down_weight, (((1,), (1,)), ((), ())), preferred_element_type=jnp.float32
        ).astype(jnp.bfloat16),
        "dp",
        scatter_dimension=0,
        tiled=True,
    )
    replicas = lax.axis_size("rep")
    replica_terms = pseudo_grad[0].astype(jnp.float32)
    average = (
        lax.psum_scatter(
            replica_terms.astype(jnp.bfloat16), "rep", scatter_dimension=0, tiled=True
        ).astype(jnp.float32)
        / replicas
    )
    new_momentum = momentum_rate * momentum + average
    step_share = (outer_rate * (average + momentum_rate * new_momentum)).astype(jnp.bfloat16)
    outer_step = lax.all_gather(step_share, "rep", axis=0, tiled=True)
    return (layer_out[None], hidden_grad[None], new_momentum, outer_step)


def solution(mesh):
    return jax.shard_map(
        per_device,
        mesh=mesh,
        in_specs=(
            P("rep", None, "tp"),
            P("tp", "dp"),
            P("rep", "tp", "dp"),
            P("rep", "tp", "dp"),
            P(("tp", "rep"), "dp"),
        ),
        out_specs=(
            P("rep", "tp", "dp"),
            P("rep", "dp", "tp"),
            P(("tp", "rep"), "dp"),
            P("tp", "dp"),
        ),
        check_vma=False,
    )
```

profile of v0, /device:TPU:0, one launch (start us, length us, event | category | flops | bytes accessed | tf_op | source)
XLA Modules:
  0.0 610.3 jit_solution(9170276419713844570)
XLA Ops:
  8.0 0.0 reduce-scatter.8.cloned.1.call-start
  8.0 0.7 reduce-scatter.8.cloned.1.call-update
  8.7 0.0 all-gather.6.cloned.1.call-start
  8.8 0.5 all-gather.6.cloned.1.call-update
  9.3 0.0 all-gather.4.cloned.1.call-start
  9.4 214.8 %reduce-scatter.8.cloned.1.call-done = bf16[1792,2048]{1,0:T(8,128)(2,1)} async-done(((bf16[7168,2048]{1,0:T(8,128)(2,1)}), bf16[1792,2048]{1,0:T(8,128)(2,1)}) %reduce-scatter.8.cloned.1.call-update) | async-done | bytes 7340048 | tf_op jit(solution)/shard_map/reduce_scatter | solution.py:33
  224.1 15.4 %multiply_convert_fusion = (bf16[1792,2048]{1,0:T(8,128)(2,1)}, f32[1792,2048]{1,0:T(8,128)}) fusion(bf16[1792,2048]{1,0:T(8,128)(2,1)} %reduce-scatter.8.cloned.1.call-done, f32[1792,2048]{1,0:T(8,128)} %param.9), kind=kLoop, calls=%fused_computation | loop fusion | flops 29360128 | bytes 44040192 | tf_op jit(solution)/shard_map/convert_element_type | solution.py:39
  239.5 0.0 all-gather.4.cloned.1.call-update
  239.5 0.0 reduce-scatter.4.cloned.1.call-start
  239.6 24.8 %fusion.3 = bf16[512,2048]{1,0:T(8,128)(2,1)} fusion(bf16[7168,2048]{1,0:T(8,128)(2,1)} %param.6, bf16[1,512,7168]{2,1,0:T(8,128)(2,1)} %param.5), kind=kOutput, calls=%fused_computation.6 | convolution fusion | flops 15033434112 | bytes 38797312 | tf_op jit(solution)/shard_map/dot_general | solution.py:15
  264.4 0.0 reduce-scatter.4.cloned.1.call-update
  264.4 0.0 reduce-scatter.6.cloned.1.call-start
  264.5 0.0 all-gather.6.cloned.1.call-done
  264.5 23.1 %convolution_convert_fusion = bf16[512,7168]{1,0:T(8,128)(2,1)} fusion(bf16[7168,2048]{1,0:T(8,128)(2,1)} %param.6, bf16[1,512,2048]{2,1,0:T(8,128)(2,1)} %all-gather.6.cloned.1.call-done), kind=kOutput, calls=%fused_computation.3 | convolution fusion | flops 15036055552 | bytes 38797312 | tf_op jit(solution)/shard_map/dot_general | solution.py:23
  287.6 0.0 reduce-scatter.6.cloned.1.call-update
  287.6 129.9 %all-gather.4.cloned.1.call-done = bf16[7168,2048]{1,0:T(8,128)(2,1)} async-done(((bf16[1792,2048]{1,0:T(8,128)(2,1)}), bf16[7168,2048]{1,0:T(8,128)(2,1)}) %all-gather.4.cloned.1.call-update) | async-done | bytes 29360144 | tf_op jit(solution)/shard_map/all_gather | solution.py:40
  417.5 34.5 %reduce-scatter.4.cloned.1.call-done = bf16[256,2048]{1,0:T(8,128)(2,1)} async-done(((bf16[512,2048]{1,0:T(8,128)(2,1)}), bf16[256,2048]{1,0:T(8,128)(2,1)}) %reduce-scatter.4.cloned.1.call-update) | async-done | bytes 1048592 | tf_op jit(solution)/shard_map/reduce_scatter | solution.py:14
  452.0 130.6 %reduce-scatter.6.cloned.1.call-done = bf16[128,7168]{1,0:T(8,128)(2,1)} async-done(((bf16[512,7168]{1,0:T(8,128)(2,1)}), bf16[128,7168]{1,0:T(8,128)(2,1)}) %reduce-scatter.6.cloned.1.call-update) | async-done | bytes 1835024 | tf_op jit(solution)/shard_map/reduce_scatter | solution.py:22
  582.7 20.1 %copy.10 = bf16[7168,2048]{1,0:T(8,128)(2,1)} copy(bf16[7168,2048]{1,0:T(8,128)(2,1)} %all-gather.4.cloned.1.call-done) | data formatting | bytes 58720256
Async XLA Ops:
  8.0 216.1 %reduce-scatter.8.cloned.1.call-start = ((), (), s32[]{:S(2)}) async-start(), calls=%async_computation.5 | async-start | bytes 36700160 | tf_op jit(solution)/shard_map/reduce_scatter | solution.py:33
  8.7 255.8 %all-gather.6.cloned.1.call-start = ((), (), s32[]{:S(2)}) async-start(), calls=%async_computation.7 | async-start | bytes 3145728 | tf_op jit(solution)/shard_map/all_gather | solution.py:20
  9.3 408.2 %all-gather.4.cloned.1.call-start = ((), (), s32[]{:S(2)}) async-start(), calls=%async_computation.6 | async-start | bytes 36700160 | tf_op jit(solution)/shard_map/all_gather | solution.py:40
  239.5 212.5 %reduce-scatter.4.cloned.1.call-start = ((), (), s32[]{:S(2)}) async-start(), calls=%async_computation.3 | async-start | bytes 3145728 | tf_op jit(solution)/shard_map/reduce_scatter | solution.py:14
  264.4 318.3 %reduce-scatter.6.cloned.1.call-start = ((), (), s32[]{:S(2)}) async-start(), calls=%async_computation.4 | async-start | bytes 9175040 | tf_op jit(solution)/shard_map/reduce_scatter | solution.py:22
Sparse Core Ops, SparseCore 0:
  11.4 212.6 reduce-scatter.7
Sparse Core Ops, SparseCore 1:
  10.8 35.7 all-gather.5
  239.6 177.8 all-gather.3
  420.2 31.8 reduce-scatter.3
  454.9 127.7 reduce-scatter.5
where the time goes:
time: 610 us
  waiting for transfers between devices  511 us (84%)
  matrix products  47.9 us (8%)
  local copies, waits for them, and re-layouts  20.1 us (3%)
  between operations  15.7 us (3%)
  other arithmetic  15.4 us (3%)
    reduce_scatter x1, waiting for transfers between devices, per_device(): lax.psum_scatter(replica_terms.astype(jnp.bfloat16), 'rep', scatter_dimen...  215 us
    reduce_scatter x1, waiting for transfers between devices, per_device(): lax.psum_scatter(lax.dot_general(row_block, down_weight, (((1,), (1,)), (...  131 us
    all_gather x1, waiting for transfers between devices, per_device(): outer_step = lax.all_gather(step_share, 'rep', axis=0, tiled=True)  130 us
    reduce_scatter x1, waiting for transfers between devices, per_device(): lax.psum_scatter(jnp.dot(row_block, down_weight, preferred_element_type=j...  34.5 us
    dot_general x1, matrix products, per_device(): jnp.dot(row_block, down_weight, preferred_element_type=jnp.float32)  24.8 us
    dot_general x1, matrix products, per_device(): lax.dot_general(row_block, down_weight, (((1,), (1,)), ((), ())), preferr...  23.1 us
    unnamed x1, local copies, waits for them, and re-layouts  20.1 us
    convert_element_type x1, other arithmetic, per_device(): (outer_rate * (average + momentum_rate * new_momentum)).astype(jnp.bfloat16)  15.4 us
  transfers between devices with their start and end apart: 5, of which 4 were waited for; matrix products, arithmetic and copies ran while one was open for 10% of the time, Pallas kernels for 0%

commit v1 on v0

--- a/solution.py
+++ b/solution.py
@@ -37,7 +37,12 @@
     )
     new_momentum = momentum_rate * momentum + average
     step_share = (outer_rate * (average + momentum_rate * new_momentum)).astype(jnp.bfloat16)
-    outer_step = lax.all_gather(step_share, "rep", axis=0, tiled=True)
+    ring = [step_share]
+    for hop in range(3):
+        ring.append(lax.ppermute(ring[-1], "rep", [(dev, (dev + 1) % 4) for dev in range(4)]))
+    outer_step = jnp.roll(
+        jnp.concatenate(ring[::-1], axis=0), (lax.axis_index("rep") + 1) * ring[0].shape[0], axis=0
+    )
     return (layer_out[None], hidden_grad[None], new_momentum, outer_step)
 
 

time: 610 us -> 569 us (0.933)
  waiting for transfers between devices: 511 us -> 415 us
  local copies, waits for them, and re-layouts: 20.1 us -> 77.5 us
    ppermute x0 -> x3, waiting for transfers between devices: none -> 199 us  [per_device(): lax.ppermute(ring[-1], 'rep', [(dev, (dev + 1) % 4) for dev in range(4)])]
    reduce_scatter x1, waiting for transfers between devices: 131 us -> 0.01 us  [per_device(): lax.psum_scatter(lax.dot_general(row_block, down_weight, (((1,), (1,)), (...]
    all_gather x1 -> x0, waiting for transfers between devices: 130 us -> none  [per_device(): outer_step = lax.all_gather(step_share, 'rep', axis=0, tiled=True)]
    reduce_scatter x1, waiting for transfers between devices: 34.5 us -> 0.01 us  [per_device(): lax.psum_scatter(jnp.dot(row_block, down_weight, preferred_element_type=j...]
    unnamed x1 -> x13, local copies, waits for them, and re-layouts: 20.1 us -> 52.7 us
    dynamic_slice x0 -> x1, local copies, waits for them, and re-layouts: none -> 20.5 us  [per_device(): jnp.roll(jnp.concatenate(ring[::-1], axis=0), (lax.axis_index('rep') + 1)...]
  transfers between devices with their start and end apart: 5 -> 7, of which waited for: 4 -> 4; matrix products, arithmetic and copies ran while one was open for 10% -> 21% of each run, Pallas kernels for 0% -> 0%
where the time goes in v1:
time: 569 us; the launch traced here: 568 us
  waiting for transfers between devices  415 us (73%)
  local copies, waits for them, and re-layouts  77.5 us (14%)
  matrix products  46.6 us (8%)
  between operations  15.7 us (3%)
  other arithmetic  13.4 us (2%)
    reduce_scatter x1, waiting for transfers between devices, per_device(): lax.psum_scatter(replica_terms.astype(jnp.bfloat16), 'rep', scatter_dimen...  215 us
    ppermute x3, waiting for transfers between devices, per_device(): lax.ppermute(ring[-1], 'rep', [(dev, (dev + 1) % 4) for dev in range(4)])  199 us
    unnamed x13, local copies, waits for them, and re-layouts  52.7 us
    dot_general x1, matrix products, per_device(): jnp.dot(row_block, down_weight, preferred_element_type=jnp.float32)  23.8 us
    dot_general x1, matrix products, per_device(): lax.dot_general(row_block, down_weight, (((1,), (1,)), ((), ())), preferr...  22.8 us
    dynamic_slice x1, local copies, waits for them, and re-layouts, per_device(): jnp.roll(jnp.concatenate(ring[::-1], axis=0), (lax.axis_index('rep') + 1)...  20.5 us
    convert_element_type x1, other arithmetic, per_device(): (outer_rate * (average + momentum_rate * new_momentum)).astype(jnp.bfloat16)  13.4 us
  transfers between devices with their start and end apart: 7, of which 4 were waited for; matrix products, arithmetic and copies ran while one was open for 21% of the time, Pallas kernels for 0%

profile of v1, /device:TPU:0, one launch (start us, length us, event | category | flops | bytes accessed | tf_op | source)
XLA Modules:
  0.0 568.4 jit_solution(3590842486752241648)
XLA Ops:
  8.0 0.0 reduce-scatter.8.cloned.1.call-start
  8.0 0.7 reduce-scatter.8.cloned.1.call-update
  8.7 0.0 all-gather.3.cloned.1.call-start
  8.8 215.4 %reduce-scatter.8.cloned.1.call-done = bf16[1792,2048]{1,0:T(8,128)(2,1)} async-done(((bf16[7168,2048]{1,0:T(8,128)(2,1)}), bf16[1792,2048]{1,0:T(8,128)(2,1)}) %reduce-scatter.8.cloned.1.call-update) | async-done | bytes 7340048 | tf_op jit(solution)/shard_map/reduce_scatter | solution.py:33
  224.1 13.4 %multiply_convert_fusion = (bf16[1792,2048]{1,0:T(8,128)(2,1)S(1)}, f32[1792,2048]{1,0:T(8,128)}) fusion(bf16[1792,2048]{1,0:T(8,128)(2,1)} %reduce-scatter.8.cloned.1.call-done, f32[1792,2048]{1,0:T(8,128)} %param.9), kind=kLoop, calls=%fused_computation | loop fusion | flops 29360128 | bytes 44040192 | tf_op jit(solution)/shard_map/convert_element_type | solution.py:39
  237.6 0.0 copy-start
  237.6 3.0 copy-done
  240.6 0.0 collective-permute-start
  240.6 81.7 %collective-permute-done = bf16[1792,2048]{1,0:T(8,128)(2,1)} collective-permute-done((bf16[1792,2048]{1,0:T(8,128)(2,1)S(1)}, bf16[1792,2048]{1,0:T(8,128)(2,1)}, u32[]{:S(2)}, u32[]{:S(2)}) %collective-permute-start) | collective-permute-done | bytes 7340064 | tf_op jit(solution)/shard_map/ppermute | solution.py:42
  322.4 0.0 collective-permute-start.1
  322.4 0.0 all-gather.3.cloned.1.call-update
  322.4 0.0 reduce-scatter.4.cloned.1.call-start
  322.5 23.8 %fusion.3 = bf16[512,2048]{1,0:T(8,128)(2,1)} fusion(bf16[7168,2048]{1,0:T(8,128)(2,1)} %param.6, bf16[1,512,7168]{2,1,0:T(8,128)(2,1)} %param.5), kind=kOutput, calls=%fused_computation.6 | convolution fusion | flops 15033434112 | bytes 38797312 | tf_op jit(solution)/shard_map/dot_general | solution.py:15
  346.3 0.0 reduce-scatter.4.cloned.1.call-update
  346.3 0.0 reduce-scatter.6.cloned.1.call-start
  346.3 58.0 %collective-permute-done.1 = bf16[1792,2048]{1,0:T(8,128)(2,1)} collective-permute-done((bf16[1792,2048]{1,0:T(8,128)(2,1)}, bf16[1792,2048]{1,0:T(8,128)(2,1)}, u32[]{:S(2)}, u32[]{:S(2)}) %collective-permute-start.1) | collective-permute-done | bytes 7340064 | tf_op jit(solution)/shard_map/ppermute | solution.py:42
  404.3 0.0 collective-permute-start.2
  404.3 0.0 all-gather.3.cloned.1.call-done
  404.3 22.8 %convolution_convert_fusion = bf16[512,7168]{1,0:T(8,128)(2,1)} fusion(bf16[7168,2048]{1,0:T(8,128)(2,1)} %param.6, bf16[1,512,2048]{2,1,0:T(8,128)(2,1)} %all-gather.3.cloned.1.call-done), kind=kOutput, calls=%fused_computation.3 | convolution fusion | flops 15036055552 | bytes 38797312 | tf_op jit(solution)/shard_map/dot_general | solution.py:23
  427.1 0.0 reduce-scatter.6.cloned.1.call-update
  427.1 59.1 %collective-permute-done.2 = bf16[1792,2048]{1,0:T(8,128)(2,1)} collective-permute-done((bf16[1792,2048]{1,0:T(8,128)(2,1)}, bf16[1792,2048]{1,0:T(8,128)(2,1)}, u32[]{:S(2)}, u32[]{:S(2)}) %collective-permute-start.2) | collective-permute-done | bytes 7340064 | tf_op jit(solution)/shard_map/ppermute | solution.py:42
  486.3 7.4 %constant_dynamic-update-slice_fusion.7 = bf16[14336,2048]{1,0:T(8,128)(2,1)} fusion(bf16[1792,2048]{1,0:T(8,128)(2,1)} %collective-permute-done.2), kind=kLoop, calls=%fused_computation.15 | loop fusion | bytes 14680064
  493.7 0.0 slice-start
  493.7 7.7 %constant_dynamic-update-slice_fusion.6 = bf16[14336,2048]{1,0:T(8,128)(2,1)} fusion(bf16[14336,2048]{1,0:T(8,128)(2,1)} %constant_dynamic-update-slice_fusion.7, bf16[1792,2048]{1,0:T(8,128)(2,1)} %collective-permute-done.1), kind=kLoop, calls=%fused_computation.14 | loop fusion | bytes 14680064
  501.5 0.0 slice-start.1
  501.5 7.6 %constant_dynamic-update-slice_fusion.5 = bf16[14336,2048]{1,0:T(8,128)(2,1)} fusion(bf16[14336,2048]{1,0:T(8,128)(2,1)} %constant_dynamic-update-slice_fusion.6, bf16[1792,2048]{1,0:T(8,128)(2,1)} %collective-permute-done), kind=kLoop, calls=%fused_computation.13 | loop fusion | bytes 14680064
  509.1 0.0 slice-done
  509.1 0.0 slice-done.1
  509.1 4.4 constant_dynamic-update-slice_fusion.4
  513.4 7.6 %constant_dynamic-update-slice_fusion.3 = bf16[14336,2048]{1,0:T(8,128)(2,1)} fusion(bf16[14336,2048]{1,0:T(8,128)(2,1)} %constant_dynamic-update-slice_fusion.4, bf16[1792,2048]{1,0:T(8,128)(2,1)} %collective-permute-done.2), kind=kLoop, calls=%fused_computation.11 | loop fusion | bytes 14680064
  521.0 7.5 %constant_dynamic-update-slice_fusion.2 = bf16[14336,2048]{1,0:T(8,128)(2,1)} fusion(bf16[14336,2048]{1,0:T(8,128)(2,1)} %constant_dynamic-update-slice_fusion.3, bf16[1792,2048]{1,0:T(8,128)(2,1)} %collective-permute-done.1), kind=kLoop, calls=%fused_computation.10 | loop fusion | bytes 14680064
  528.5 7.5 %constant_dynamic-update-slice_fusion.1 = bf16[14336,2048]{1,0:T(8,128)(2,1)} fusion(bf16[14336,2048]{1,0:T(8,128)(2,1)} %constant_dynamic-update-slice_fusion.2, bf16[1792,2048]{1,0:T(8,128)(2,1)} %collective-permute-done), kind=kLoop, calls=%fused_computation.9 | loop fusion | bytes 14680064
  536.0 4.3 constant_dynamic-update-slice_fusion
  540.3 20.5 %constant_dynamic-slice_fusion = bf16[7168,2048]{1,0:T(8,128)(2,1)} fusion(bf16[14336,2048]{1,0:T(8,128)(2,1)} %constant_dynamic-update-slice_fusion, s32[]{:T(128)S(6)} %select_n.14), kind=kLoop, calls=%fused_computation.16 | loop fusion | bytes 58720260 | tf_op jit(solution)/shard_map/jit(_roll_dynamic)/dynamic_slice | solution.py:43
  560.8 0.0 reduce-scatter.4.cloned.1.call-done
  560.8 0.0 reduce-scatter.6.cloned.1.call-done
  (1 shorter events, 0.0 us)
Async XLA Ops:
  8.0 216.1 %reduce-scatter.8.cloned.1.call-start = ((), (), s32[]{:S(2)}) async-start(), calls=%async_computation.5 | async-start | bytes 36700160 | tf_op jit(solution)/shard_map/reduce_scatter | solution.py:33
  8.7 395.6 %all-gather.3.cloned.1.call-start = ((), (), s32[]{:S(2)}) async-start(), calls=%async_computation.6 | async-start | bytes 3145728 | tf_op jit(solution)/shard_map/all_gather | solution.py:20
  237.6 3.0 copy-start
  240.6 81.7 %collective-permute-start = (bf16[1792,2048]{1,0:T(8,128)(2,1)S(1)}, bf16[1792,2048]{1,0:T(8,128)(2,1)}, u32[]{:S(2)}, u32[]{:S(2)}) collective-permute-start(bf16[1792,2048]{1,0:T(8,128)(2,1)S(1)} %get-tuple-element.4), channel_id=1, source_target_pairs={{0,8},{8,16},{16,24},{24,0},{1,9},{9,17},{17,25},{25,1},{2,10},{10... | collective-permute-start | bytes 22020104 | tf_op jit(solution)/shard_map/ppermute | solution.py:42
  322.4 82.0 %collective-permute-start.1 = (bf16[1792,2048]{1,0:T(8,128)(2,1)}, bf16[1792,2048]{1,0:T(8,128)(2,1)}, u32[]{:S(2)}, u32[]{:S(2)}) collective-permute-start(bf16[1792,2048]{1,0:T(8,128)(2,1)} %collective-permute-done), channel_id=1, source_target_pairs={{0,8},{8,16},{16,24},{24,0},{1,9},{9,17},{17,25},{25,1},{2,10},{10... | collective-permute-start | bytes 22020104 | tf_op jit(solution)/shard_map/ppermute | solution.py:42
  322.4 238.4 %reduce-scatter.4.cloned.1.call-start = ((), (), s32[]{:S(2)}) async-start(), calls=%async_computation.3 | async-start | bytes 3145728 | tf_op jit(solution)/shard_map/reduce_scatter | solution.py:14
  346.3 214.5 %reduce-scatter.6.cloned.1.call-start = ((), (), s32[]{:S(2)}) async-start(), calls=%async_computation.4 | async-start | bytes 9175040 | tf_op jit(solution)/shard_map/reduce_scatter | solution.py:22
  404.3 82.0 %collective-permute-start.2 = (bf16[1792,2048]{1,0:T(8,128)(2,1)}, bf16[1792,2048]{1,0:T(8,128)(2,1)}, u32[]{:S(2)}, u32[]{:S(2)}) collective-permute-start(bf16[1792,2048]{1,0:T(8,128)(2,1)} %collective-permute-done.1), channel_id=1, source_target_pairs={{0,8},{8,16},{16,24},{24,0},{1,9},{9,17},{17,25},{25,1},{2,10},{10... | collective-permute-start | bytes 22020104 | tf_op jit(solution)/shard_map/ppermute | solution.py:42
  493.7 15.4 %slice-start = ((s8[7340032]{0:T(1024)(128)(4,1)}), s8[4194304]{0:T(1024)(128)(4,1)S(1)}, s32[]{:S(2)}) async-start(s8[7340032]{0:T(1024)(128)(4,1)} %bitcast.13), calls=%async_computation.7 | async-start | bytes 8388608
  501.5 7.6 %slice-start.1 = ((s8[7340032]{0:T(1024)(128)(4,1)}), s8[3145728]{0:T(1024)(128)(4,1)S(1)}, s32[]{:S(2)}) async-start(s8[7340032]{0:T(1024)(128)(4,1)} %bitcast.13), calls=%async_computation.8 | async-start | bytes 6291456
Sparse Core Ops, SparseCore 0:
  11.4 212.6 reduce-scatter.7
Sparse Core Ops, SparseCore 1:
  322.5 34.1 all-gather.2
  359.3 31.8 reduce-scatter.3
  427.2 128.8 reduce-scatter.5
